TPU v7x, 128 devices: a whole 4x4x4 slice. The times are simulated.
128 devices in a mesh: tok: 8 (over y, z_lo), hid: 16 (over z_hi, x, core).
Axes of the slice: x: 4, y: 4, z: 4 (z_hi: 2, z_lo: 2; z = z_hi * 2 + z_lo), core: 2. Of those that a mesh axis runs over, the one named last changes fastest.
Arguments:
- tokens: bfloat16 [12288, 6144], P('tok', 'hid'), may hold values from -6 to 6
- cotangent: bfloat16 [12288, 6144], P('tok', 'hid'), may hold values from -6 to 6
- expert_choice: int32 [12288, 2], P('tok'), may hold values from 0 to 7, as said below
- router: bfloat16 [8, 6144], replicated, may hold values from -0.078125 to 0.078125
- gate_up: bfloat16 [6144, 2, 8192], P('tok', None, 'hid'), may hold values from -0.109375 to 0.109375
- w_down: bfloat16 [6144, 8192], P('tok', 'hid'), may hold values from -0.0625 to 0.0625
Outputs:
- grad_tokens: bfloat16 [12288, 6144], P('tok', 'hid')
- d_combine: float32 [12288, 2], P('tok')
- d_gate_up: float32 [6144, 2, 8192], P('tok', None, 'hid')
- d_down: float32 [6144, 8192], P('tok', 'hid')
Inputs may be any that keep to these rules, and one draw needn't show every extreme that they name: `expert_choice`: each row names 2 different experts. In every aligned block of 1536 rows at most 432 rows name expert 0 and at least half of 432 do; some block has exactly 432.
All inputs are finite; a program needn't handle non-finite values.
Results may differ from a plain program's by a relative error of at most 0.017.
Values may be sent and summed in bfloat16 or wider, within the bound.
A program may use at most 128 MiB of HBM per device.

v0:
```python
import jax
import jax.numpy as jnp
from jax import lax
from jax.sharding import Mesh
from jax.sharding import PartitionSpec as P

CAP = 432
TOK = ("y", "zl")
ALL = ("y", "zl", "hid")


def swap_pairs():
    pairs = []
    for y in range(4):
        for zl in range(2):
            for h in range(16):
                to_y, to_h = (h // 4, y * 4 + h % 4)
                pairs.append(((y * 2 + zl) * 16 + h, (to_y * 2 + zl) * 16 + to_h))
    return pairs


def silu_pair(pre):
    sigma = jax.nn.sigmoid(pre)
    return (pre * sigma, sigma * (1.0 + pre * (1.0 - sigma)))


def dot_f32(left, right, dims):
    return lax.dot_general(
        left, right, ((dims[0], dims[1]), ((), ())), preferred_element_type=jnp.float32
    )


def local(tokens, cotangent, expert_choice, router, gate_up, w_down):
    cols = tokens.shape[1]
    rows_own, hid = w_down.shape
    zl = lax.axis_index("zl")
    first = expert_choice[:, 0]
    second = expert_choice[:, 1]
    in_first = first == 0
    in_second = second == 0
    routed = jnp.logical_or(in_first, in_second)
    flags = routed.astype(jnp.int32)
    slot_rank = jnp.cumsum(flags) - flags
    slot_ids = jnp.arange(CAP, dtype=jnp.int32)
    placed = jnp.logical_and(routed[None, :], slot_rank[None, :] == slot_ids[:, None])
    select = placed.astype(jnp.bfloat16)
    weights = jnp.concatenate([gate_up.reshape(rows_own, 2 * hid), w_down], axis=1)
    other_weights = lax.ppermute(weights, "zl", [(0, 1), (1, 0)])
    dispatched = dot_f32(select, jnp.concatenate([tokens, cotangent], axis=1), ((1,), (0,)))
    moved = lax.ppermute(dispatched.astype(jnp.bfloat16), ALL, swap_pairs())
    gathered = lax.all_gather(moved, "hid", axis=0)
    router_cols = lax.dynamic_slice_in_dim(router, lax.axis_index("hid") * cols, cols, 1)
    logits = dot_f32(tokens, router_cols, ((1,), (1,)))
    other = first + second
    labels = jnp.arange(logits.shape[1], dtype=jnp.int32)
    other_logit = jnp.sum(jnp.where(other[:, None] == labels[None, :], logits, 0.0), axis=1)
    margin_part = jnp.sum(jnp.where(placed, (logits[:, 0] - other_logit)[None, :], 0.0), axis=1)
    margin = lax.psum(margin_part, "hid")
    filled = jnp.any(placed, axis=1)
    slot_gate = jnp.where(filled, jax.nn.sigmoid(margin), 0.0)
    parts = gathered.reshape(4, 4, CAP, 2, cols).transpose(3, 0, 2, 1, 4)
    parts = parts.reshape(2, 4 * CAP, 4 * cols)
    rows_in, rows_cot = (parts[0], parts[1])
    low = jnp.where(zl == 0, weights, other_weights)
    high = jnp.where(zl == 0, other_weights, weights)
    both = jnp.concatenate([low, high], axis=0)
    w_gu = both[:, : 2 * hid]
    w_d = both[:, 2 * hid :]
    pre = jnp.concatenate(
        [
            dot_f32(rows_in, w_gu, ((1,), (0,))).astype(jnp.bfloat16),
            dot_f32(rows_cot, w_d, ((1,), (0,))).astype(jnp.bfloat16),
        ],
        axis=1,
    )
    pre = lax.psum_scatter(pre, "y", scatter_dimension=0, tiled=True).astype(jnp.float32)
    gate_pre, up_pre, raw = (pre[:, :hid], pre[:, hid : 2 * hid], pre[:, 2 * hid :])
    active, slope = silu_pair(gate_pre)
    product = active * up_pre
    scale = slot_gate[:, None]
    score_part = jnp.sum(product * raw, axis=1)
    upstream = scale * raw
    mids = jnp.concatenate(
        [
            (upstream * up_pre * slope).astype(jnp.bfloat16),
            (upstream * active).astype(jnp.bfloat16),
            (scale * product).astype(jnp.bfloat16),
        ],
        axis=1,
    )
    mids = lax.all_gather(mids, "y", axis=0, tiled=True)
    mid_gu, mid_d = (mids[:, : 2 * hid], mids[:, 2 * hid :])
    scores = lax.psum(score_part, "hid")
    back = dot_f32(mid_gu, w_gu, ((1,), (1,))).astype(jnp.bfloat16)
    back = back.reshape(4, CAP, 4, cols).transpose(0, 2, 1, 3).reshape(16, CAP, cols)
    back = lax.psum_scatter(back, "hid", scatter_dimension=0, tiled=False)

    def grads_of(rows):
        return jnp.concatenate(
            [
                dot_f32(lax.dynamic_slice_in_dim(rows_in, rows, rows_own, 1), mid_gu, ((0,), (0,))),
                dot_f32(lax.dynamic_slice_in_dim(rows_cot, rows, rows_own, 1), mid_d, ((0,), (0,))),
            ],
            axis=1,
        )

    sent = grads_of((1 - zl) * rows_own).astype(jnp.bfloat16)
    arrived = lax.ppermute(sent, "zl", [(0, 1), (1, 0)])
    grads = grads_of(zl * rows_own) + arrived.astype(jnp.float32)
    back = lax.ppermute(back, ALL, swap_pairs())
    grad_tokens = dot_f32(select, back, ((0,), (0,))).astype(jnp.bfloat16)
    token_score = jnp.sum(jnp.where(placed, scores[:, None], 0.0), axis=0)
    d_combine = jnp.stack(
        [jnp.where(in_first, token_score, 0.0), jnp.where(in_second, token_score, 0.0)], axis=1
    )
    d_gate_up = grads[:, : 2 * hid].reshape(rows_own, 2, hid)
    d_down = grads[:, 2 * hid :]
    return (grad_tokens, d_combine, d_gate_up, d_down)


def solution(mesh):
    split = Mesh(mesh.devices.reshape(4, 2, mesh.shape["hid"]), ("y", "zl", "hid"))
    return jax.shard_map(
        local,
        mesh=split,
        in_specs=(
            P(TOK, "hid"),
            P(TOK, "hid"),
            P(TOK, None),
            P(),
            P(TOK, None, "hid"),
            P(TOK, "hid"),
        ),
        out_specs=(P(TOK, "hid"), P(TOK, None), P(TOK, None, "hid"), P(TOK, "hid")),
        check_vma=False,
    )
```

profile of v0, /device:TPU:24, one launch (start us, length us, event | category | flops | bytes accessed | tf_op | source)
XLA Modules:
  0.0 526.6 jit_solution(5789460973194179525)
XLA Ops:
  7.2 0.0 all-gather.6.cloned.1.call-start
  7.2 0.8 convert_reduce_fusion
  8.1 0.3 reduce-window.9
  8.3 0.1 slice.67
  8.4 0.1 slice_reduce_fusion
  8.6 0.1 bitcast_subtract_fusion
  8.7 3.1 fusion.33
  11.8 7.9 %collective-permute-start = (bf16[432,768]{1,0:T(8,128)(2,1)S(1)}, bf16[432,768]{1,0:T(8,128)(2,1)S(1)}, u32[]{:S(2)}, u32[]{:S(2)}) collective-permute-start(bf16[432,768]{1,0:T(8,128)(2,1)S(1)} %fusion.33), channel_id=1, source_target_pairs={{0,0},{1,1},{2,2},{3,3},{4,32},{5,33},{6,34},{7,35},{8,64},{9,65},... | collective-permute-start | bytes 1990664 | tf_op jit(solution)/shard_map/ppermute | solution.py:50
  19.7 16.6 %collective-permute-done = bf16[432,768]{1,0:T(8,128)(2,1)S(1)} collective-permute-done((bf16[432,768]{1,0:T(8,128)(2,1)S(1)}, bf16[432,768]{1,0:T(8,128)(2,1)S(1)}, u32[]{:S(2)}, u32[]{:S(2)}) %collective-permute-start) | collective-permute-done | bytes 663584 | tf_op jit(solution)/shard_map/ppermute | solution.py:50
  36.3 0.8 copy-done.10
  37.2 0.0 all-gather.6.cloned.1.call-update
  37.2 0.0 reduce-scatter.3.cloned.1.call-start
  37.3 0.4 copy.23
  37.7 0.1 constant_dynamic-update-slice_fusion.1
  37.8 0.6 copy-done.9
  38.4 0.1 constant_dynamic-update-slice_fusion
  38.5 2.2 collective-permute-start.1
  40.6 76.6 %collective-permute-done.1 = bf16[768,1536]{1,0:T(8,128)(2,1)} collective-permute-done((bf16[768,1536]{1,0:T(8,128)(2,1)S(1)}, bf16[768,1536]{1,0:T(8,128)(2,1)}, u32[]{:S(2)}, u32[]{:S(2)}) %collective-permute-start.1) | collective-permute-done | bytes 2359328 | tf_op jit(solution)/shard_map/ppermute | solution.py:48
  117.3 4.2 broadcast_select_fusion.1
  121.5 18.0 %all-gather.6.cloned.1.call-done = bf16[6912,768]{1,0:T(8,128)(2,1)} async-done(((bf16[432,768]{1,0:T(8,128)(2,1)}), bf16[6912,768]{1,0:T(8,128)(2,1)}) %all-gather.6.cloned.1.call-update) | async-done | bytes 10616848 | tf_op jit(solution)/shard_map/all_gather | solution.py:51
  139.5 20.7 %reshape.96 = bf16[4,4,432,2,384]{4,3,2,1,0:T(2,128)(2,1)} reshape(bf16[6912,768]{1,0:T(8,128)(2,1)} %all-gather.6.cloned.1.call-done) | data formatting | bytes 21233664 | tf_op jit(solution)/shard_map/reshape | solution.py:61
  160.1 8.5 %copy.26 = bf16[4,4,432,2,384]{4,1,2,0,3:T(4,128)(2,1)S(1)} copy(bf16[4,4,432,2,384]{4,3,2,1,0:T(2,128)(2,1)} %reshape.96) | data formatting | bytes 21233664 | tf_op jit(solution)/shard_map/reshape | solution.py:61
  168.7 3.8 fusion.53
  172.5 1.0 copy.22
  173.5 1.0 copy.24
  174.5 1.7 copy-done.2
  176.2 0.7 copy-done.4
  176.9 2.4 copy-done.6
  179.3 6.1 %convolution_convert_fusion.1 = bf16[1728,1024]{1,0:T(8,128)(2,1)S(1)} fusion(bf16[1728,1536]{1,0:T(8,128)(2,1)S(1)} %bitcast.29, bf16[768,1536]{1,0:T(8,128)(2,1)S(1)} %copy-done.4, bf16[768,1536]{1,0:T(8,128)(2,1)S(1)} %copy-done.6), kind=kOutput, calls=%fused_computation.6 | convolution fusion | flops 5443878912 | bytes 13565952 | tf_op jit(solution)/shard_map/dot_general | solution.py:28
  185.4 3.1 convolution_convert_fusion.2
  188.5 2.8 pad_maximum_fusion
  191.3 0.0 reduce-scatter.3.cloned.1.call-update
  191.3 0.0 all-gather.4.cloned.1.call-start
  191.4 1.2 copy-done.8
  192.6 0.4 select_reduce_fusion.2
  193.0 0.4 fusion.16
  193.5 52.6 %reduce-scatter.3.cloned.1.call-done = bf16[432,1536]{1,0:T(8,128)(2,1)} async-done(((bf16[1728,1536]{1,0:T(8,128)(2,1)}), bf16[432,1536]{1,0:T(8,128)(2,1)}) %reduce-scatter.3.cloned.1.call-update) | async-done | bytes 1327120 | tf_op jit(solution)/shard_map/reduce_scatter | solution.py:76
  246.1 1.6 convert_element_type.51
  247.8 0.3 multiply_reduce_fusion
  248.1 37.8 %psum.15 = f32[432]{0:T(512)S(1)} all-reduce(f32[432]{0:T(512)S(1)} %multiply_reduce_fusion), channel_id=1, replica_groups=mesh['y'=4,'zl'=2,'hid'=16] {'hid'}, use_global_device_ids=true, to_apply=%region_9.10 | all-reduce | flops 432 | bytes 3456 | tf_op jit(solution)/shard_map/psum | solution.py:93
  285.9 1.0 select_reduce_fusion
  286.9 33.4 %psum.14 = f32[432]{0:T(512)S(1)} all-reduce(f32[432]{0:T(512)S(1)} %get-tuple-element.5), channel_id=1, replica_groups=mesh['y'=4,'zl'=2,'hid'=16] {'hid'}, use_global_device_ids=true, to_apply=%region_5.6 | all-reduce | flops 432 | bytes 3456 | tf_op jit(solution)/shard_map/psum | solution.py:58
  320.3 0.6 multiply_convert_fusion.2
  320.9 1.1 pad_maximum_fusion.4
  322.1 0.0 reduce-scatter.5.cloned.1.call-start
  322.1 53.0 %all-gather.4.cloned.1.call-done = bf16[1728,1536]{1,0:T(8,128)(2,1)} async-done(((bf16[432,1536]{1,0:T(8,128)(2,1)}), bf16[1728,1536]{1,0:T(8,128)(2,1)}) %all-gather.4.cloned.1.call-update) | async-done | bytes 5308432 | tf_op jit(solution)/shard_map/all_gather | solution.py:91
  375.1 9.7 %convolution_convert_fusion = bf16[1728,1536]{1,0:T(8,128)(2,1)} fusion(bf16[1728,1536]{1,0:T(8,128)(2,1)} %all-gather.4.cloned.1.call-done, bf16[768,1536]{1,0:T(8,128)(2,1)S(1)} %copy-done.5, bf16[768,1536]{1,0:T(8,128)(2,1)} %get-tuple-element.11), kind=kOutput, calls=%fused_computation.1 | convolution fusion | flops 5444763648 | bytes 13565952 | tf_op jit(solution)/shard_map/dot_general | solution.py:28
  384.9 9.7 %reshape.98 = bf16[4,432,4,384]{3,2,1,0:T(4,128)(2,1)} reshape(bf16[1728,1536]{1,0:T(8,128)(2,1)} %convolution_convert_fusion) | data formatting | bytes 10616832 | tf_op jit(solution)/shard_map/reshape | solution.py:95
  394.6 5.5 %copy.17 = bf16[4,432,4,384]{3,1,2,0:T(8,128)(2,1)} copy(bf16[4,432,4,384]{3,2,1,0:T(4,128)(2,1)} %reshape.98) | data formatting | bytes 10616832 | tf_op jit(solution)/shard_map/reshape | solution.py:95
  400.1 4.0 fusion.28
  404.2 5.1 fusion.20
  409.4 1.6 pad_maximum_fusion.1
  411.0 1.7 collective-permute-start.3
  412.7 0.6 pad_maximum_fusion.5
  413.3 4.4 fusion.9
  417.7 7.1 %fusion.3 = f32[768,1024]{1,0:T(8,128)} fusion(bf16[1728,1536]{1,0:T(8,128)(2,1)} %all-gather.4.cloned.1.call-done, bf16[1728,1536]{1,0:T(8,128)(2,1)S(1)} %bitcast.35, s32[]{:T(128)S(6)} %select_n.58), kind=kOutput, calls=%fused_computation.12 | convolution fusion | flops 2717908992 | bytes 9338884 | tf_op jit(solution)/shard_map/dot_general | solution.py:28
  424.8 75.8 %reduce-scatter.5.cloned.1.call-done = bf16[1,432,384]{2,1,0:T(8,128)(2,1)} async-done(((bf16[16,432,384]{2,1,0:T(8,128)(2,1)}), bf16[1,432,384]{2,1,0:T(8,128)(2,1)}) %reduce-scatter.5.cloned.1.call-update) | async-done | bytes 331792 | tf_op jit(solution)/shard_map/reduce_scatter | solution.py:96
  500.6 3.8 collective-permute-start.2
  504.4 3.4 maximum_add_fusion
  507.8 0.3 slice.79
  508.1 1.3 slice.80
  509.3 3.7 reshape.100
  513.1 3.9 collective-permute-done.2
  517.0 3.1 convolution_convert_fusion.3
  (37 shorter events, 0.2 us)
Async XLA Ops:
  7.2 184.2 %copy-start = (bf16[8,6144]{1,0:T(8,128)(2,1)S(1)}, bf16[8,6144]{1,0:T(8,128)(2,1)}, u32[]{:S(2)}) copy-start(bf16[8,6144]{1,0:T(8,128)(2,1)} %param.9) | copy-start | bytes 294916
  7.2 132.3 %all-gather.6.cloned.1.call-start = ((), (), s32[]{:S(2)}) async-start(), calls=%async_computation.5 | async-start | bytes 11280384 | tf_op jit(solution)/shard_map/all_gather | solution.py:51
  8.7 28.6 %copy-start.7 = (bf16[768,2,512]{2,1,0:T(2,128)(2,1)S(1)}, bf16[768,2,512]{2,1,0:T(2,128)(2,1)}, u32[]{:S(2)}) copy-start(bf16[768,2,512]{2,1,0:T(2,128)(2,1)} %param.10) | copy-start | bytes 4718596
  11.8 24.6 %collective-permute-start = (bf16[432,768]{1,0:T(8,128)(2,1)S(1)}, bf16[432,768]{1,0:T(8,128)(2,1)S(1)}, u32[]{:S(2)}, u32[]{:S(2)}) collective-permute-start(bf16[432,768]{1,0:T(8,128)(2,1)S(1)} %fusion.33), channel_id=1, source_target_pairs={{0,0},{1,1},{2,2},{3,3},{4,32},{5,33},{6,34},{7,35},{8,64},{9,65},... | collective-permute-start | bytes 1990664 | tf_op jit(solution)/shard_map/ppermute | solution.py:50
  36.3 0.8 copy-start.10
  37.2 208.9 %reduce-scatter.3.cloned.1.call-start = ((), (), s32[]{:S(2)}) async-start(), calls=%async_computation.2 | async-start | bytes 6635520 | tf_op jit(solution)/shard_map/reduce_scatter | solution.py:76
  37.3 1.1 copy-start.9
  38.5 78.8 %collective-permute-start.1 = (bf16[768,1536]{1,0:T(8,128)(2,1)S(1)}, bf16[768,1536]{1,0:T(8,128)(2,1)}, u32[]{:S(2)}, u32[]{:S(2)}) collective-permute-start(bf16[768,1536]{1,0:T(8,128)(2,1)S(1)} %constant_dynamic-update-slice_fusion), channel_id=1, source_target_pairs={{0,16},{16,0},{1,17},{17,1},{2,18},{18,2},{3,19},{19,3},{4,20},{20... | collective-permute-start | bytes 7077896 | tf_op jit(solution)/shard_map/ppermute | solution.py:48
  173.5 2.7 copy-start.2
  173.5 3.4 copy-start.4
  173.5 5.8 %copy-start.6 = (bf16[768,1536]{1,0:T(8,128)(2,1)S(1)}, bf16[768,1536]{1,0:T(8,128)(2,1)}, u32[]{:S(2)}) copy-start(bf16[768,1536]{1,0:T(8,128)(2,1)} %get-tuple-element.11) | copy-start | bytes 7077892
  174.5 10.9 %copy-start.3 = (bf16[216,8,4,384]{3,1,2,0:T(8,128)(2,1)}, bf16[216,8,4,384]{3,1,2,0:T(8,128)(2,1)S(1)}, u32[]{:S(2)}) copy-start(bf16[216,8,4,384]{3,1,2,0:T(8,128)(2,1)S(1)} %copy.24) | copy-start | bytes 15925252
  191.3 1.3 copy-start.8
  191.3 183.8 %all-gather.4.cloned.1.call-start = ((), (), s32[]{:S(2)}) async-start(), calls=%async_computation.3 | async-start | bytes 6635520 | tf_op jit(solution)/shard_map/all_gather | solution.py:91
  320.9 54.3 %copy-start.5 = (bf16[768,1536]{1,0:T(8,128)(2,1)S(1)}, bf16[768,1536]{1,0:T(8,128)(2,1)}, u32[]{:S(2)}) copy-start(bf16[768,1536]{1,0:T(8,128)(2,1)} %get-tuple-element.10) | copy-start | bytes 7077892
  322.1 178.5 %reduce-scatter.5.cloned.1.call-start = ((), (), s32[]{:S(2)}) async-start(), calls=%async_computation.4 | async-start | bytes 5640192 | tf_op jit(solution)/shard_map/reduce_scatter | solution.py:96
  400.1 4.1 slice-start
  400.1 4.1 slice-start.1
  409.3 3.3 copy-start.11
  409.4 8.4 %slice-start.2 = ((s8[5308416]{0:T(1024)(128)(4,1)}), s8[1114112]{0:T(1024)(128)(4,1)S(1)}, s32[]{:S(2)}) async-start(s8[5308416]{0:T(1024)(128)(4,1)} %bitcast.33), calls=%async_computation.8 | async-start | bytes 2228224
  411.0 93.4 %collective-permute-start.3 = (bf16[768,1536]{1,0:T(8,128)(2,1)}, bf16[768,1536]{1,0:T(8,128)(2,1)}, u32[]{:S(2)}, u32[]{:S(2)}) collective-permute-start(bf16[768,1536]{1,0:T(8,128)(2,1)} %pad_maximum_fusion.1), channel_id=1, source_target_pairs={{0,16},{16,0},{1,17},{17,1},{2,18},{18,2},{3,19},{19,3},{4,20},{20... | collective-permute-start | bytes 7077896 | tf_op jit(solution)/shard_map/ppermute | solution.py:108
  413.3 4.4 slice-start.3
  500.6 16.4 %collective-permute-start.2 = (bf16[432,384]{1,0:T(8,128)(2,1)}, bf16[432,384]{1,0:T(8,128)(2,1)}, u32[]{:S(2)}, u32[]{:S(2)}) collective-permute-start(bf16[432,384]{1,0:T(8,128)(2,1)} %bitcast.41), channel_id=1, source_target_pairs={{0,0},{1,1},{2,2},{3,3},{4,32},{5,33},{6,34},{7,35},{8,64},{9,65},... | collective-permute-start | bytes 995336 | tf_op jit(solution)/shard_map/ppermute | solution.py:110
  509.3 10.7 %copy-start.1 = (bf16[8,6144]{1,0:T(8,128)(2,1)S(1)}, bf16[8,6144]{1,0:T(8,128)(2,1)}, u32[]{:S(2)}) copy-start(bf16[8,6144]{1,0:T(8,128)(2,1)} %param.9) | copy-start | bytes 294916
Sparse Core Ops, SparseCore 0:
  37.3 102.1 all-gather.5
  191.5 54.6 reduce-scatter.2
  322.2 52.9 all-gather.3
  400.2 100.3 reduce-scatter.4
where the time goes:
time: 528 us; the launch traced here: 527 us
  waiting for transfers between devices  297 us (56%)
  blocking collectives  71.2 us (13%)
  local copies, waits for them, and re-layouts  63.7 us (12%)
  matrix products  46.2 us (9%)
  other arithmetic  19.1 us (4%)
  starting transfers between devices  15.7 us (3%)
  between operations  14.1 us (3%)
    ppermute x1, waiting for transfers between devices, local(): other_weights = lax.ppermute(weights, 'zl', [(0, 1), (1, 0)])  76.6 us
    reduce_scatter x1, waiting for transfers between devices, local(): back = lax.psum_scatter(back, 'hid', scatter_dimension=0, tiled=False)  75.8 us
    all_gather x1, waiting for transfers between devices, local(): mids = lax.all_gather(mids, 'y', axis=0, tiled=True)  53 us
    reduce_scatter x1, waiting for transfers between devices, local(): lax.psum_scatter(pre, 'y', scatter_dimension=0, tiled=True)  52.6 us
    dot_general x10, matrix products, dot_f32(): lax.dot_general(left, right, ((dims[0], dims[1]), ((), ())), preferred_el...  46.2 us
    psum x1, blocking collectives, local(): scores = lax.psum(score_part, 'hid')  37.8 us
    psum x1, blocking collectives, local(): margin = lax.psum(margin_part, 'hid')  33.4 us
    reshape x2, local copies, waits for them, and re-layouts, local(): parts = gathered.reshape(4, 4, CAP, 2, cols).transpose(3, 0, 2, 1, 4)  29.2 us
  transfers between devices with their start and end apart: 8, of which 7 were waited for; matrix products, arithmetic and copies ran while one was open for 7% of the time, Pallas kernels for 0%

commit v1 on v0

--- a/solution.py
+++ b/solution.py
@@ -55,7 +55,12 @@
     labels = jnp.arange(logits.shape[1], dtype=jnp.int32)
     other_logit = jnp.sum(jnp.where(other[:, None] == labels[None, :], logits, 0.0), axis=1)
     margin_part = jnp.sum(jnp.where(placed, (logits[:, 0] - other_logit)[None, :], 0.0), axis=1)
-    margin = lax.psum(margin_part, "hid")
+
+    def view_kinds(my_data):
+        block_last = jax.lax.all_gather(my_data, "hid").sum(axis=0)
+        return block_last
+
+    margin = view_kinds(margin_part)
     filled = jnp.any(placed, axis=1)
     slot_gate = jnp.where(filled, jax.nn.sigmoid(margin), 0.0)
     parts = gathered.reshape(4, 4, CAP, 2, cols).transpose(3, 0, 2, 1, 4)

time: 528 us -> 560 us (1.061)
  blocking collectives: 71.2 us -> 103 us
    unnamed x0 -> x1, blocking collectives: none -> 65.2 us
    psum x1 -> x0, blocking collectives: 33.4 us -> none  [local(): margin = lax.psum(margin_part, 'hid')]
where the time goes in v1:
time: 560 us; the launch traced here: 559 us
  waiting for transfers between devices  295 us (53%)
  blocking collectives  103 us (18%)
  local copies, waits for them, and re-layouts  64.6 us (12%)
  matrix products  46.2 us (8%)
  other arithmetic  19.1 us (3%)
  starting transfers between devices  15.7 us (3%)
  between operations  14.8 us (3%)
    ppermute x1, waiting for transfers between devices, local(): other_weights = lax.ppermute(weights, 'zl', [(0, 1), (1, 0)])  76.6 us
    reduce_scatter x1, waiting for transfers between devices, local(): back = lax.psum_scatter(back, 'hid', scatter_dimension=0, tiled=False)  75.7 us
    unnamed x1, blocking collectives  65.2 us
    all_gather x1, waiting for transfers between devices, local(): mids = lax.all_gather(mids, 'y', axis=0, tiled=True)  53.1 us
    reduce_scatter x1, waiting for transfers between devices, local(): lax.psum_scatter(pre, 'y', scatter_dimension=0, tiled=True)  51.4 us
    dot_general x10, matrix products, dot_f32(): lax.dot_general(left, right, ((dims[0], dims[1]), ((), ())), preferred_el...  46.2 us
    psum x1, blocking collectives, local(): scores = lax.psum(score_part, 'hid')  37.8 us
    reshape x2, local copies, waits for them, and re-layouts, local(): parts = gathered.reshape(4, 4, CAP, 2, cols).transpose(3, 0, 2, 1, 4)  29.2 us
  transfers between devices with their start and end apart: 8, of which 7 were waited for; matrix products, arithmetic and copies ran while one was open for 7% of the time, Pallas kernels for 0%

profile of v1, /device:TPU:24, one launch (start us, length us, event | category | flops | bytes accessed | tf_op | source)
XLA Modules:
  0.0 558.8 jit_solution(11049082813256234120)
XLA Ops:
  7.2 0.8 convert_reduce_fusion
  8.1 0.3 reduce-window.9
  8.3 0.1 slice.67
  8.4 0.1 slice_reduce_fusion
  8.6 0.1 bitcast_subtract_fusion
  8.7 3.1 fusion.33
  11.8 7.9 %collective-permute-start = (bf16[432,768]{1,0:T(8,128)(2,1)S(1)}, bf16[432,768]{1,0:T(8,128)(2,1)S(1)}, u32[]{:S(2)}, u32[]{:S(2)}) collective-permute-start(bf16[432,768]{1,0:T(8,128)(2,1)S(1)} %fusion.33), channel_id=1, source_target_pairs={{0,0},{1,1},{2,2},{3,3},{4,32},{5,33},{6,34},{7,35},{8,64},{9,65},... | collective-permute-start | bytes 1990664 | tf_op jit(solution)/shard_map/ppermute | solution.py:50
  19.7 16.6 %collective-permute-done = bf16[432,768]{1,0:T(8,128)(2,1)S(1)} collective-permute-done((bf16[432,768]{1,0:T(8,128)(2,1)S(1)}, bf16[432,768]{1,0:T(8,128)(2,1)S(1)}, u32[]{:S(2)}, u32[]{:S(2)}) %collective-permute-start) | collective-permute-done | bytes 663584 | tf_op jit(solution)/shard_map/ppermute | solution.py:50
  36.3 0.8 copy-done.10
  37.2 0.0 reduce-scatter.3.cloned.1.call-start
  37.3 0.4 copy.23
  37.7 0.1 constant_dynamic-update-slice_fusion.1
  37.8 0.6 copy-done.9
  38.4 0.1 constant_dynamic-update-slice_fusion
  38.5 2.2 collective-permute-start.1
  40.6 76.6 %collective-permute-done.1 = bf16[768,1536]{1,0:T(8,128)(2,1)} collective-permute-done((bf16[768,1536]{1,0:T(8,128)(2,1)S(1)}, bf16[768,1536]{1,0:T(8,128)(2,1)}, u32[]{:S(2)}, u32[]{:S(2)}) %collective-permute-start.1) | collective-permute-done | bytes 2359328 | tf_op jit(solution)/shard_map/ppermute | solution.py:48
  117.3 4.2 broadcast_select_fusion.1
  121.5 18.0 %all-gather.7.cloned.1.call-done = bf16[6912,768]{1,0:T(8,128)(2,1)} async-done(((bf16[432,768]{1,0:T(8,128)(2,1)}), bf16[6912,768]{1,0:T(8,128)(2,1)}) %all-gather.7.cloned.1.call-update) | async-done | bytes 10616848 | tf_op jit(solution)/shard_map/all_gather | solution.py:51
  139.5 20.7 %reshape.104 = bf16[4,4,432,2,384]{4,3,2,1,0:T(2,128)(2,1)} reshape(bf16[6912,768]{1,0:T(8,128)(2,1)} %all-gather.7.cloned.1.call-done) | data formatting | bytes 21233664 | tf_op jit(solution)/shard_map/reshape | solution.py:66
  160.1 8.5 %copy.26 = bf16[4,4,432,2,384]{4,1,2,0,3:T(4,128)(2,1)S(1)} copy(bf16[4,4,432,2,384]{4,3,2,1,0:T(2,128)(2,1)} %reshape.104) | data formatting | bytes 21233664 | tf_op jit(solution)/shard_map/reshape | solution.py:66
  168.7 3.8 fusion.53
  172.5 1.0 copy.22
  173.5 1.0 copy.24
  174.5 1.7 copy-done.2
  176.2 0.7 copy-done.4
  176.9 2.4 copy-done.6
  179.3 6.1 %convolution_convert_fusion.1 = bf16[1728,1024]{1,0:T(8,128)(2,1)S(1)} fusion(bf16[1728,1536]{1,0:T(8,128)(2,1)S(1)} %bitcast.30, bf16[768,1536]{1,0:T(8,128)(2,1)S(1)} %copy-done.4, bf16[768,1536]{1,0:T(8,128)(2,1)S(1)} %copy-done.6), kind=kOutput, calls=%fused_computation.6 | convolution fusion | flops 5443878912 | bytes 13565952 | tf_op jit(solution)/shard_map/dot_general | solution.py:28
  185.4 3.1 convolution_convert_fusion.2
  188.5 2.8 pad_maximum_fusion
  191.3 0.0 all-gather.5.cloned.1.call-start
  191.4 1.2 copy-done.8
  192.6 0.4 select_reduce_fusion.2
  193.1 0.6 dynamic-slice
  194.3 0.4 fusion.16
  194.7 51.4 %reduce-scatter.3.cloned.1.call-done = bf16[432,1536]{1,0:T(8,128)(2,1)} async-done(((bf16[1728,1536]{1,0:T(8,128)(2,1)}), bf16[432,1536]{1,0:T(8,128)(2,1)}) %reduce-scatter.3.cloned.1.call-update) | async-done | bytes 1327120 | tf_op jit(solution)/shard_map/reduce_scatter | solution.py:81
  246.1 1.6 convert_element_type.51
  247.8 0.3 multiply_reduce_fusion
  248.1 37.8 %psum.7 = f32[432]{0:T(512)S(1)} all-reduce(f32[432]{0:T(512)S(1)} %multiply_reduce_fusion), channel_id=1, replica_groups=mesh['y'=4,'zl'=2,'hid'=16] {'hid'}, use_global_device_ids=true, to_apply=%region_9.10 | all-reduce | flops 432 | bytes 3456 | tf_op jit(solution)/shard_map/psum | solution.py:98
  285.9 1.0 select_reduce_fusion
  286.9 0.3 dynamic-update-slice
  287.2 65.2 %all-reduce = f32[6912]{0:T(1024)S(1)} all-reduce(f32[6912]{0:T(1024)S(1)} %dynamic-update-slice), channel_id=2, replica_groups=mesh['y'=4,'zl'=2,'hid'=16] {'hid'}, use_global_device_ids=true, to_apply=%add | all-reduce | flops 6912 | bytes 55296
  352.3 0.1 reshape.110
  352.5 0.6 multiply_convert_fusion.2
  353.1 1.1 pad_maximum_fusion.4
  354.2 0.0 reduce-scatter.5.cloned.1.call-start
  354.3 53.1 %all-gather.5.cloned.1.call-done = bf16[1728,1536]{1,0:T(8,128)(2,1)} async-done(((bf16[432,1536]{1,0:T(8,128)(2,1)}), bf16[1728,1536]{1,0:T(8,128)(2,1)}) %all-gather.5.cloned.1.call-update) | async-done | bytes 5308432 | tf_op jit(solution)/shard_map/all_gather | solution.py:96
  407.4 9.7 %convolution_convert_fusion = bf16[1728,1536]{1,0:T(8,128)(2,1)} fusion(bf16[1728,1536]{1,0:T(8,128)(2,1)} %all-gather.5.cloned.1.call-done, bf16[768,1536]{1,0:T(8,128)(2,1)S(1)} %copy-done.5, bf16[768,1536]{1,0:T(8,128)(2,1)} %get-tuple-element.11), kind=kOutput, calls=%fused_computation.1 | convolution fusion | flops 5444763648 | bytes 13565952 | tf_op jit(solution)/shard_map/dot_general | solution.py:28
  417.1 9.7 %reshape.106 = bf16[4,432,4,384]{3,2,1,0:T(4,128)(2,1)} reshape(bf16[1728,1536]{1,0:T(8,128)(2,1)} %convolution_convert_fusion) | data formatting | bytes 10616832 | tf_op jit(solution)/shard_map/reshape | solution.py:100
  426.9 5.5 copy.17
  432.4 4.0 fusion.28
  436.4 5.1 fusion.20
  441.6 1.6 pad_maximum_fusion.1
  443.2 1.7 collective-permute-start.3
  444.9 0.6 pad_maximum_fusion.5
  445.5 4.4 fusion.9
  450.0 7.1 %fusion.3 = f32[768,1024]{1,0:T(8,128)} fusion(bf16[1728,1536]{1,0:T(8,128)(2,1)} %all-gather.5.cloned.1.call-done, bf16[1728,1536]{1,0:T(8,128)(2,1)S(1)} %bitcast.36, s32[]{:T(128)S(6)} %select_n.62), kind=kOutput, calls=%fused_computation.12 | convolution fusion | flops 2717908992 | bytes 9338884 | tf_op jit(solution)/shard_map/dot_general | solution.py:28
  457.0 75.7 %reduce-scatter.5.cloned.1.call-done = bf16[1,432,384]{2,1,0:T(8,128)(2,1)} async-done(((bf16[16,432,384]{2,1,0:T(8,128)(2,1)}), bf16[1,432,384]{2,1,0:T(8,128)(2,1)}) %reduce-scatter.5.cloned.1.call-update) | async-done | bytes 331792 | tf_op jit(solution)/shard_map/reduce_scatter | solution.py:101
  532.7 3.8 collective-permute-start.2
  536.5 3.4 maximum_add_fusion
  539.9 0.3 slice.79
  540.3 1.3 slice.80
  541.5 3.7 reshape.108
  545.2 3.9 collective-permute-done.2
  549.2 3.1 convolution_convert_fusion.3
  (44 shorter events, 0.3 us)
Async XLA Ops:
  7.2 184.2 %copy-start = (bf16[8,6144]{1,0:T(8,128)(2,1)S(1)}, bf16[8,6144]{1,0:T(8,128)(2,1)}, u32[]{:S(2)}) copy-start(bf16[8,6144]{1,0:T(8,128)(2,1)} %param.9) | copy-start | bytes 294916
  7.2 132.3 %all-gather.7.cloned.1.call-start = ((), (), s32[]{:S(2)}) async-start(), calls=%async_computation.5 | async-start | bytes 11280384 | tf_op jit(solution)/shard_map/all_gather | solution.py:51
  8.7 28.6 %copy-start.7 = (bf16[768,2,512]{2,1,0:T(2,128)(2,1)S(1)}, bf16[768,2,512]{2,1,0:T(2,128)(2,1)}, u32[]{:S(2)}) copy-start(bf16[768,2,512]{2,1,0:T(2,128)(2,1)} %param.10) | copy-start | bytes 4718596
  11.8 24.6 %collective-permute-start = (bf16[432,768]{1,0:T(8,128)(2,1)S(1)}, bf16[432,768]{1,0:T(8,128)(2,1)S(1)}, u32[]{:S(2)}, u32[]{:S(2)}) collective-permute-start(bf16[432,768]{1,0:T(8,128)(2,1)S(1)} %fusion.33), channel_id=1, source_target_pairs={{0,0},{1,1},{2,2},{3,3},{4,32},{5,33},{6,34},{7,35},{8,64},{9,65},... | collective-permute-start | bytes 1990664 | tf_op jit(solution)/shard_map/ppermute | solution.py:50
  36.3 0.8 copy-start.10
  37.2 208.9 %reduce-scatter.3.cloned.1.call-start = ((), (), s32[]{:S(2)}) async-start(), calls=%async_computation.2 | async-start | bytes 6635520 | tf_op jit(solution)/shard_map/reduce_scatter | solution.py:81
  37.3 1.1 copy-start.9
  38.5 78.8 %collective-permute-start.1 = (bf16[768,1536]{1,0:T(8,128)(2,1)S(1)}, bf16[768,1536]{1,0:T(8,128)(2,1)}, u32[]{:S(2)}, u32[]{:S(2)}) collective-permute-start(bf16[768,1536]{1,0:T(8,128)(2,1)S(1)} %constant_dynamic-update-slice_fusion), channel_id=1, source_target_pairs={{0,16},{16,0},{1,17},{17,1},{2,18},{18,2},{3,19},{19,3},{4,20},{20... | collective-permute-start | bytes 7077896 | tf_op jit(solution)/shard_map/ppermute | solution.py:48
  173.5 2.7 copy-start.2
  173.5 3.4 copy-start.4
  173.5 5.8 %copy-start.6 = (bf16[768,1536]{1,0:T(8,128)(2,1)S(1)}, bf16[768,1536]{1,0:T(8,128)(2,1)}, u32[]{:S(2)}) copy-start(bf16[768,1536]{1,0:T(8,128)(2,1)} %get-tuple-element.11) | copy-start | bytes 7077892
  174.5 10.9 %copy-start.3 = (bf16[216,8,4,384]{3,1,2,0:T(8,128)(2,1)}, bf16[216,8,4,384]{3,1,2,0:T(8,128)(2,1)S(1)}, u32[]{:S(2)}) copy-start(bf16[216,8,4,384]{3,1,2,0:T(8,128)(2,1)S(1)} %copy.24) | copy-start | bytes 15925252
  191.3 1.3 copy-start.8
  191.3 1.7 copy-start.12
  191.3 216.0 %all-gather.5.cloned.1.call-start = ((), (), s32[]{:S(2)}) async-start(), calls=%async_computation.3 | async-start | bytes 6635520 | tf_op jit(solution)/shard_map/all_gather | solution.py:96
  353.1 54.3 %copy-start.5 = (bf16[768,1536]{1,0:T(8,128)(2,1)S(1)}, bf16[768,1536]{1,0:T(8,128)(2,1)}, u32[]{:S(2)}) copy-start(bf16[768,1536]{1,0:T(8,128)(2,1)} %get-tuple-element.10) | copy-start | bytes 7077892
  354.2 178.5 %reduce-scatter.5.cloned.1.call-start = ((), (), s32[]{:S(2)}) async-start(), calls=%async_computation.4 | async-start | bytes 5640192 | tf_op jit(solution)/shard_map/reduce_scatter | solution.py:101
  432.3 4.1 slice-start
  432.3 4.1 slice-start.1
  441.6 3.3 copy-start.11
  441.6 8.4 %slice-start.2 = ((s8[5308416]{0:T(1024)(128)(4,1)}), s8[1114112]{0:T(1024)(128)(4,1)S(1)}, s32[]{:S(2)}) async-start(s8[5308416]{0:T(1024)(128)(4,1)} %bitcast.34), calls=%async_computation.8 | async-start | bytes 2228224
  443.2 93.3 %collective-permute-start.3 = (bf16[768,1536]{1,0:T(8,128)(2,1)}, bf16[768,1536]{1,0:T(8,128)(2,1)}, u32[]{:S(2)}, u32[]{:S(2)}) collective-permute-start(bf16[768,1536]{1,0:T(8,128)(2,1)} %pad_maximum_fusion.1), channel_id=1, source_target_pairs={{0,16},{16,0},{1,17},{17,1},{2,18},{18,2},{3,19},{19,3},{4,20},{20... | collective-permute-start | bytes 7077896 | tf_op jit(solution)/shard_map/ppermute | solution.py:113
  445.5 4.4 slice-start.3
  532.7 16.4 %collective-permute-start.2 = (bf16[432,384]{1,0:T(8,128)(2,1)}, bf16[432,384]{1,0:T(8,128)(2,1)}, u32[]{:S(2)}, u32[]{:S(2)}) collective-permute-start(bf16[432,384]{1,0:T(8,128)(2,1)} %bitcast.42), channel_id=1, source_target_pairs={{0,0},{1,1},{2,2},{3,3},{4,32},{5,33},{6,34},{7,35},{8,64},{9,65},... | collective-permute-start | bytes 995336 | tf_op jit(solution)/shard_map/ppermute | solution.py:115
  541.5 10.7 %copy-start.1 = (bf16[8,6144]{1,0:T(8,128)(2,1)S(1)}, bf16[8,6144]{1,0:T(8,128)(2,1)}, u32[]{:S(2)}) copy-start(bf16[8,6144]{1,0:T(8,128)(2,1)} %param.9) | copy-start | bytes 294916
Sparse Core Ops, SparseCore 0:
  37.3 102.1 all-gather.6
  191.5 54.6 reduce-scatter.2
  354.4 52.9 all-gather.4
  432.5 100.2 reduce-scatter.4
